TPU v7x, 32 devices: a whole 2x2x4 slice. The times are simulated.
32 devices in a mesh: ao: 8 (over y, x, core), aux: 4 (over z).
Axes of the slice: x: 2, y: 2, z: 4, core: 2. Of those that a mesh axis runs over, the one named last changes fastest.
Arguments:
- blocks: bfloat16 [48, 256, 128, 128], P('ao', 'aux'), may hold values from -6 to 6
- pairs: int32 [48, 2], P('ao'), may hold values from 0 to 79, as said below
- counts: int32 [8], P('ao'), may hold values from 1 to 6, as said below
- owned_blocks: int32 [80], P('ao'), may hold values from 0 to 79, as said below
- occ_coef: bfloat16 [80, 8, 128], P('ao'), may hold values from -0.5 to 0.5
- vir_coef: bfloat16 [10240, 9216], P('ao', 'aux'), may hold values from -0.109375 to 0.109375
Outputs:
- b_tensor: bfloat16 [256, 8, 9216], P('ao', None, 'aux')
Inputs may be any that keep to these rules, and one draw needn't show every extreme that they name: `pairs`: among the used slots of one ao index, at most 3 have nu blocks whose rows one owner holds; in every draw some index reaches 3. `counts`: some ao index uses all 6 slots in every draw. `owned_blocks`: every atom block appears exactly once.
All inputs are finite; a program needn't handle non-finite values.
Results may differ from a plain program's by a relative error of at most 0.014.
Values may be sent and summed in bfloat16 or wider, within the bound.
A program may use at most 128 MiB of HBM per device.

v0:
```python
import jax
import jax.numpy as jnp
from jax import lax
from jax.sharding import PartitionSpec as P


def block_place(block_ids, owned_all):
    hits = block_ids[..., None] == owned_all
    positions = jnp.arange(owned_all.shape[0], dtype=jnp.int32)
    return jnp.sum(jnp.where(hits, positions, 0), axis=-1)


def per_device(blocks, pairs, counts, owned_blocks, occ_coef, vir_coef):
    groups = lax.axis_size("ao")
    own_index = lax.axis_index("ao")
    slot_count = blocks.shape[0]
    aux_depth = blocks.shape[1]
    block_width = blocks.shape[3]
    occupied = occ_coef.shape[1]
    all_pairs, all_counts, all_owned = (
        lax.all_gather(pairs, "ao", axis=0, tiled=True),
        lax.all_gather(counts, "ao", axis=0, tiled=True),
        lax.all_gather(owned_blocks, "ao", axis=0, tiled=True),
    )
    occ_all = lax.all_gather(occ_coef, "ao", axis=0, tiled=True)
    total_blocks = all_owned.shape[0]
    per_owner = total_blocks // groups
    slot_ids = jnp.arange(slot_count, dtype=jnp.int32)
    in_use = slot_ids < counts[0]
    occ_pick = occ_all[block_place(pairs[:, 0], all_owned)]
    slab_values = jnp.einsum("sim,spmn->spin", occ_pick, blocks, preferred_element_type=jnp.float32)
    slab_values = jnp.where(in_use[:, None, None, None], slab_values, 0.0).astype(jnp.bfloat16)
    flat_slabs = slab_values.reshape(slot_count, aux_depth * occupied, block_width)
    place_all = block_place(all_pairs[:, 1], all_owned).reshape(groups, slot_count)
    owner_all = place_all // per_owner
    local_all = place_all % per_owner
    live_all = slot_ids[None, :] < all_counts[:, None]
    mine_all = live_all & (owner_all == own_index)
    local_ids = jnp.arange(per_owner, dtype=jnp.int32)
    slabs_got = lax.all_gather(flat_slabs, "ao", axis=0, tiled=True)
    assign = (
        mine_all.reshape(-1)[None, :] & (local_all.reshape(-1)[None, :] == local_ids[:, None])
    ).astype(jnp.bfloat16)
    summed = jnp.einsum("lt,tqm->qlm", assign, slabs_got, preferred_element_type=jnp.float32)
    rows_local = summed.reshape(summed.shape[0], per_owner * block_width).astype(jnp.bfloat16)
    rows_whole = lax.all_gather(rows_local, "aux", axis=0, tiled=True)
    share = rows_whole.shape[0] // groups
    result = lax.psum_scatter(
        jnp.dot(rows_whole, vir_coef, preferred_element_type=jnp.float32).astype(jnp.bfloat16),
        "ao",
        scatter_dimension=0,
        tiled=True,
    ).astype(jnp.float32)
    return result.reshape(share // occupied, occupied, vir_coef.shape[1]).astype(jnp.bfloat16)


def solution(mesh):
    in_specs = (
        P("ao", "aux", None, None),
        P("ao", None),
        P("ao"),
        P("ao"),
        P("ao", None, None),
        P("ao", "aux"),
    )
    out_specs = P("ao", None, "aux")
    return jax.shard_map(
        per_device, mesh=mesh, in_specs=in_specs, out_specs=out_specs, check_vma=False
    )
```

profile of v0, /device:TPU:0, one launch (start us, length us, event | category | flops | bytes accessed | tf_op | source)
XLA Modules:
  0.0 291.0 jit_solution(9892513670469097050)
XLA Ops:
  7.2 0.7 slice_bitcast_fusion.1
  7.9 1.3 dynamic-slice
  9.9 0.8 dynamic-update-slice.1
  10.7 0.8 dynamic-update-slice
  11.5 9.5 %all-reduce.2 = (s32[80]{0:T(128)S(1)}, s32[8]{0:T(128)S(1)}) all-reduce(s32[80]{0:T(128)S(1)} %dynamic-update-slice, s32[8]{0:T(128)S(1)} %dynamic-update-slice.1), channel_id=1, replica_groups=mesh['ao'=8,'aux'=4] {'ao'}, use_global_device_ids=true, to_apply=%add | all-reduce | flops 88 | bytes 704
  21.0 0.2 select_reduce_fusion.1
  21.2 8.6 %all_gather.18 = bf16[80,8,128]{2,1,0:T(8,128)(2,1)S(1)} all-gather(bf16[10,8,128]{2,1,0:T(8,128)(2,1)} %param.10), channel_id=1, replica_groups=mesh['ao'=8,'aux'=4] {'ao'}, dimensions={0}, use_global_device_ids=true | all-gather | bytes 184320 | tf_op jit(solution)/shard_map/all_gather | solution.py:25
  29.8 0.6 gather_fusion
  30.4 7.2 %fusion.4 = bf16[6,512,128]{2,1,0:T(8,128)(2,1)} fusion(bf16[6,64,128,128]{3,2,1,0:T(8,128)(2,1)} %param.6, pred[6]{0:T(512)(128)(4,1)S(1)} %iota_compare_fusion.2, bf16[6,8,128]{2,1,0:T(8,128)(2,1)S(1)} %gather_fusion), kind=kOutput, calls=%fused_computation.6 | convolution fusion | flops 101449728 | bytes 13381638 | tf_op jit(solution)/shard_map/sim,spmn->spin/dot_general | solution.py:31
  37.6 0.0 all-gather.4.cloned.1.call-update
  37.6 0.0 all-gather.6.cloned.1.call-start
  37.7 0.1 iota_compare_fusion.1
  37.8 0.1 lt.52
  37.9 8.6 %all-gather = s32[8,6,2]{1,2,0:T(2,128)S(1)} all-gather(s32[1,6,2]{1,2,0:T(2,128)S(1)} %bitcast.35), channel_id=1, replica_groups=mesh['ao'=8,'aux'=4] {'ao'}, dimensions={0}, use_global_device_ids=true | all-gather | bytes 432 | tf_op jit(solution)/shard_map/all_gather | solution.py:21
  46.5 0.1 reshape.75
  46.5 0.2 select_reduce_fusion
  46.8 36.7 %all-gather.4.cloned.1.call-done = bf16[48,512,128]{2,1,0:T(8,128)(2,1)} async-done(((bf16[6,512,128]{2,1,0:T(8,128)(2,1)}), bf16[48,512,128]{2,1,0:T(8,128)(2,1)}) %all-gather.4.cloned.1.call-update) | async-done | bytes 6291472 | tf_op jit(solution)/shard_map/all_gather | solution.py:40
  83.5 6.4 %convert_bitcast_fusion = bf16[512,10,128]{2,1,0:T(8,128)(2,1)S(1)} fusion(bf16[48,512,128]{2,1,0:T(8,128)(2,1)} %all-gather.4.cloned.1.call-done, s32[48]{0:T(128)S(1)} %and_select_fusion, pred[48]{0:T(512)(128)(4,1)S(1)} %compare_and_fusion), kind=kOutput, calls=%fused_computation.4 | convolution fusion | flops 63570880 | bytes 7602416 | tf_op jit(solution)/shard_map/lt,tqm->qlm/dot_general | solution.py:44
  89.9 2.6 copy.17
  92.5 0.0 all-gather.6.cloned.1.call-update
  92.5 0.2 reduce-scatter.2.cloned.1.call-start
  92.7 98.0 %all-gather.6.cloned.1.call-done = bf16[2048,1280]{0,1:T(8,128)(2,1)} async-done(((bf16[512,1280]{0,1:T(8,128)(2,1)}), bf16[2048,1280]{0,1:T(8,128)(2,1)}) %all-gather.6.cloned.1.call-update) | async-done | bytes 5242896 | tf_op jit(solution)/shard_map/all_gather | solution.py:46
  190.7 18.4 %convolution_convert_fusion = bf16[2048,2304]{1,0:T(8,128)(2,1)} fusion(bf16[2048,1280]{0,1:T(8,128)(2,1)} %all-gather.6.cloned.1.call-done, bf16[1280,2304]{1,0:T(8,128)(2,1)} %param.11), kind=kOutput, calls=%fused_computation.1 | convolution fusion | flops 12084314112 | bytes 20578304 | tf_op jit(solution)/shard_map/dot_general | solution.py:49
  209.1 75.3 %reduce-scatter.2.cloned.1.call-done = bf16[256,2304]{1,0:T(8,128)(2,1)} async-done(((bf16[2048,2304]{1,0:T(8,128)(2,1)}), bf16[256,2304]{1,0:T(8,128)(2,1)}) %reduce-scatter.2.cloned.1.call-update) | async-done | bytes 1179664 | tf_op jit(solution)/shard_map/reduce_scatter | solution.py:48
  (13 shorter events, 0.1 us)
Async XLA Ops:
  6.5 76.9 %all-gather.4.cloned.1.call-start = ((), (), s32[]{:S(2)}) async-start(), calls=%async_computation.1 | async-start | bytes 7077888 | tf_op jit(solution)/shard_map/all_gather | solution.py:40
  30.4 7.5 %copy-start = (s32[6,2]{0,1:T(2,128)S(1)}, s32[6,2]{0,1:T(2,128)}, u32[]{:S(2)}) copy-start(s32[6,2]{0,1:T(2,128)} %param.7) | copy-start | bytes 148
  37.6 153.0 %all-gather.6.cloned.1.call-start = ((), (), s32[]{:S(2)}) async-start(), calls=%async_computation.2 | async-start | bytes 6553600 | tf_op jit(solution)/shard_map/all_gather | solution.py:46
  92.5 191.9 %reduce-scatter.2.cloned.1.call-start = ((), (), s32[]{:S(2)}) async-start(), calls=%async_computation.3 | async-start | bytes 10616832 | tf_op jit(solution)/shard_map/reduce_scatter | solution.py:48
Sparse Core Ops, SparseCore 0:
  37.8 45.6 all-gather.3
  92.6 98.0 all-gather.5
  209.2 75.1 reduce-scatter.1
where the time goes:
time: 291 us
  waiting for transfers between devices  210 us (72%)
  matrix products  32.1 us (11%)
  blocking collectives  26.7 us (9%)
  between operations  14.5 us (5%)
  local copies, waits for them, and re-layouts  6.95 us (2%)
    all_gather x1, waiting for transfers between devices, per_device(): rows_whole = lax.all_gather(rows_local, 'aux', axis=0, tiled=True)  98 us
    reduce_scatter x1, waiting for transfers between devices, per_device(): lax.psum_scatter(jnp.dot(rows_whole, vir_coef, preferred_element_type=jnp...  75.3 us
    all_gather x1, waiting for transfers between devices, per_device(): slabs_got = lax.all_gather(flat_slabs, 'ao', axis=0, tiled=True)  36.7 us
    dot_general x1, matrix products, per_device(): jnp.dot(rows_whole, vir_coef, preferred_element_type=jnp.float32)  18.4 us
    unnamed x1, blocking collectives  9.49 us
    all_gather x1, blocking collectives, per_device(): occ_all = lax.all_gather(occ_coef, 'ao', axis=0, tiled=True)  8.6 us
    all_gather x1, blocking collectives, per_device(): lax.all_gather(pairs, 'ao', axis=0, tiled=True)  8.59 us
    dot_general x1, matrix products, per_device(): jnp.einsum('sim,spmn->spin', occ_pick, blocks, preferred_element_type=jnp...  7.2 us
  transfers between devices with their start and end apart: 3, of which 3 were waited for; matrix products, arithmetic and copies ran while one was open for 0% of the time, Pallas kernels for 0%

commit v1 on v0

--- a/solution.py
+++ b/solution.py
@@ -2,6 +2,17 @@
 import jax.numpy as jnp
 from jax import lax
 from jax.sharding import PartitionSpec as P
+
+
+def gather_around(value, axis, dim):
+    ways = lax.axis_size(axis)
+    pieces = [value]
+    for far in range(1, ways):
+        pieces.append(
+            lax.ppermute(pieces[far - 1], axis, [(d, (d - 1) % ways) for d in range(ways)])
+        )
+    line = jnp.concatenate(pieces, axis=dim)
+    return jnp.roll(line, lax.axis_index(axis) * value.shape[dim], axis=dim)
 
 
 def block_place(block_ids, owned_all):
@@ -43,7 +54,7 @@
     ).astype(jnp.bfloat16)
     summed = jnp.einsum("lt,tqm->qlm", assign, slabs_got, preferred_element_type=jnp.float32)
     rows_local = summed.reshape(summed.shape[0], per_owner * block_width).astype(jnp.bfloat16)
-    rows_whole = lax.all_gather(rows_local, "aux", axis=0, tiled=True)
+    rows_whole = gather_around(rows_local, "aux", 0)
     share = rows_whole.shape[0] // groups
     result = lax.psum_scatter(
         jnp.dot(rows_whole, vir_coef, preferred_element_type=jnp.float32).astype(jnp.bfloat16),

time: 291 us -> 292 us (level)
  waiting for transfers between devices: 210 us -> 196 us
  starting transfers between devices: 0.27 us -> 12.1 us
  local copies, waits for them, and re-layouts: 6.95 us -> 12.6 us
  matrix products: 32.1 us -> 28.9 us
    all_gather x1 -> x0, waiting for transfers between devices: 98 us -> none  [per_device(): rows_whole = lax.all_gather(rows_local, 'aux', axis=0, tiled=True)]
    ppermute x0 -> x3, waiting for transfers between devices: none -> 81.1 us  [gather_around(): lax.ppermute(pieces[far - 1], axis, [(d, (d - 1) % ways) for d in range(w...]
    ppermute x0 -> x3, starting transfers between devices: none -> 12 us  [gather_around(): lax.ppermute(pieces[far - 1], axis, [(d, (d - 1) % ways) for d in range(w...]
    unnamed x8 -> x19, local copies, waits for them, and re-layouts: 3.05 us -> 8.28 us
    dot_general x1, matrix products: 18.4 us -> 15.2 us  [per_device(): jnp.dot(rows_whole, vir_coef, preferred_element_type=jnp.float32)]
  transfers between devices with their start and end apart: 3 -> 5, of which waited for: 3 -> 5; matrix products, arithmetic and copies ran while one was open for 0% -> 1% of each run, Pallas kernels for 0% -> 0%
where the time goes in v1:
time: 292 us; the launch traced here: 291 us
  waiting for transfers between devices  196 us (67%)
  matrix products  28.9 us (10%)
  blocking collectives  26.7 us (9%)
  between operations  14.8 us (5%)
  local copies, waits for them, and re-layouts  12.6 us (4%)
  starting transfers between devices  12.1 us (4%)
    ppermute x3, waiting for transfers between devices, gather_around(): lax.ppermute(pieces[far - 1], axis, [(d, (d - 1) % ways) for d in range(w...  81.1 us
    reduce_scatter x1, waiting for transfers between devices, per_device(): lax.psum_scatter(jnp.dot(rows_whole, vir_coef, preferred_element_type=jnp...  77.9 us
    all_gather x1, waiting for transfers between devices, per_device(): slabs_got = lax.all_gather(flat_slabs, 'ao', axis=0, tiled=True)  36.7 us
    dot_general x1, matrix products, per_device(): jnp.dot(rows_whole, vir_coef, preferred_element_type=jnp.float32)  15.2 us
    ppermute x3, starting transfers between devices, gather_around(): lax.ppermute(pieces[far - 1], axis, [(d, (d - 1) % ways) for d in range(w...  12 us
    unnamed x1, blocking collectives  9.49 us
    all_gather x1, blocking collectives, per_device(): occ_all = lax.all_gather(occ_coef, 'ao', axis=0, tiled=True)  8.6 us
    all_gather x1, blocking collectives, per_device(): lax.all_gather(pairs, 'ao', axis=0, tiled=True)  8.59 us
  transfers between devices with their start and end apart: 5, of which 5 were waited for; matrix products, arithmetic and copies ran while one was open for 1% of the time, Pallas kernels for 0%

profile of v1, /device:TPU:0, one launch (start us, length us, event | category | flops | bytes accessed | tf_op | source)
XLA Modules:
  0.0 291.3 jit_solution(16555827852540722931)
XLA Ops:
  7.2 0.7 slice_bitcast_fusion.1
  7.9 1.3 dynamic-slice
  9.8 0.7 dynamic-update-slice.1
  10.5 0.8 dynamic-update-slice
  11.3 9.5 %all-reduce.2 = (s32[80]{0:T(128)S(1)}, s32[8]{0:T(128)S(1)}) all-reduce(s32[80]{0:T(128)S(1)} %dynamic-update-slice, s32[8]{0:T(128)S(1)} %dynamic-update-slice.1), channel_id=1, replica_groups=mesh['ao'=8,'aux'=4] {'ao'}, use_global_device_ids=true, to_apply=%add | all-reduce | flops 88 | bytes 704
  21.0 8.6 %all_gather.15 = bf16[80,8,128]{2,1,0:T(8,128)(2,1)S(1)} all-gather(bf16[10,8,128]{2,1,0:T(8,128)(2,1)} %param.10), channel_id=1, replica_groups=mesh['ao'=8,'aux'=4] {'ao'}, dimensions={0}, use_global_device_ids=true | all-gather | bytes 184320 | tf_op jit(solution)/shard_map/all_gather | solution.py:36
  29.6 0.6 gather_fusion
  30.2 7.2 %fusion.5 = bf16[6,512,128]{2,1,0:T(8,128)(2,1)} fusion(bf16[6,64,128,128]{3,2,1,0:T(8,128)(2,1)} %param.6, pred[6]{0:T(512)(128)(4,1)S(1)} %iota_compare_fusion.2, bf16[6,8,128]{2,1,0:T(8,128)(2,1)S(1)} %gather_fusion), kind=kOutput, calls=%fused_computation.7 | convolution fusion | flops 101449728 | bytes 13381638 | tf_op jit(solution)/shard_map/sim,spmn->spin/dot_general | solution.py:42
  37.6 8.6 %all-gather = s32[8,6,2]{1,2,0:T(2,128)S(1)} all-gather(s32[1,6,2]{1,2,0:T(2,128)S(1)} %bitcast.36), channel_id=1, replica_groups=mesh['ao'=8,'aux'=4] {'ao'}, dimensions={0}, use_global_device_ids=true | all-gather | bytes 432 | tf_op jit(solution)/shard_map/all_gather | solution.py:32
  46.5 36.7 %all-gather.3.cloned.1.call-done = bf16[48,512,128]{2,1,0:T(8,128)(2,1)} async-done(((bf16[6,512,128]{2,1,0:T(8,128)(2,1)}), bf16[48,512,128]{2,1,0:T(8,128)(2,1)}) %all-gather.3.cloned.1.call-update) | async-done | bytes 6291472 | tf_op jit(solution)/shard_map/all_gather | solution.py:51
  83.2 6.4 %convert_bitcast_fusion = bf16[512,10,128]{2,1,0:T(8,128)(2,1)S(1)} fusion(bf16[48,512,128]{2,1,0:T(8,128)(2,1)} %all-gather.3.cloned.1.call-done, s32[48]{0:T(128)S(1)} %and_select_fusion, pred[48]{0:T(512)(128)(4,1)S(1)} %compare_and_fusion), kind=kOutput, calls=%fused_computation.5 | convolution fusion | flops 63570880 | bytes 7602416 | tf_op jit(solution)/shard_map/lt,tqm->qlm/dot_general | solution.py:55
  89.7 1.5 copy.17
  91.2 3.4 %collective-permute-start = (bf16[512,1280]{0,1:T(8,128)(2,1)S(1)}, bf16[512,1280]{0,1:T(8,128)(2,1)S(1)}, u32[]{:S(2)}, u32[]{:S(2)}) collective-permute-start(bf16[512,1280]{0,1:T(8,128)(2,1)S(1)} %bitcast.33), channel_id=1, source_target_pairs={{0,3},{1,0},{2,1},{3,2},{4,7},{5,4},{6,5},{7,6},{8,11},{9,8},{10,9... | collective-permute-start | bytes 3932168 | tf_op jit(solution)/shard_map/ppermute | solution.py:12
  94.6 28.5 %collective-permute-done = bf16[512,1280]{0,1:T(8,128)(2,1)S(1)} collective-permute-done((bf16[512,1280]{0,1:T(8,128)(2,1)S(1)}, bf16[512,1280]{0,1:T(8,128)(2,1)S(1)}, u32[]{:S(2)}, u32[]{:S(2)}) %collective-permute-start) | collective-permute-done | bytes 1310752 | tf_op jit(solution)/shard_map/ppermute | solution.py:12
  123.0 4.3 %collective-permute-start.1 = (bf16[512,1280]{0,1:T(8,128)(2,1)S(1)}, bf16[512,1280]{0,1:T(8,128)(2,1)}, u32[]{:S(2)}, u32[]{:S(2)}) collective-permute-start(bf16[512,1280]{0,1:T(8,128)(2,1)S(1)} %collective-permute-done), channel_id=1, source_target_pairs={{0,3},{1,0},{2,1},{3,2},{4,7},{5,4},{6,5},{7,6},{8,11},{9,8},{10,9... | collective-permute-start | bytes 3932168 | tf_op jit(solution)/shard_map/ppermute | solution.py:12
  127.3 27.6 %collective-permute-done.1 = bf16[512,1280]{0,1:T(8,128)(2,1)} collective-permute-done((bf16[512,1280]{0,1:T(8,128)(2,1)S(1)}, bf16[512,1280]{0,1:T(8,128)(2,1)}, u32[]{:S(2)}, u32[]{:S(2)}) %collective-permute-start.1) | collective-permute-done | bytes 1310752 | tf_op jit(solution)/shard_map/ppermute | solution.py:12
  154.9 4.4 %collective-permute-start.2 = (bf16[512,1280]{0,1:T(8,128)(2,1)}, bf16[512,1280]{0,1:T(8,128)(2,1)}, u32[]{:S(2)}, u32[]{:S(2)}) collective-permute-start(bf16[512,1280]{0,1:T(8,128)(2,1)} %collective-permute-done.1), channel_id=1, source_target_pairs={{0,3},{1,0},{2,1},{3,2},{4,7},{5,4},{6,5},{7,6},{8,11},{9,8},{10,9... | collective-permute-start | bytes 3932168 | tf_op jit(solution)/shard_map/ppermute | solution.py:12
  159.6 1.6 constant_dynamic-update-slice_fusion.5
  161.3 25.1 %collective-permute-done.2 = bf16[512,1280]{0,1:T(8,128)(2,1)} collective-permute-done((bf16[512,1280]{0,1:T(8,128)(2,1)}, bf16[512,1280]{0,1:T(8,128)(2,1)}, u32[]{:S(2)}, u32[]{:S(2)}) %collective-permute-start.2) | collective-permute-done | bytes 1310752 | tf_op jit(solution)/shard_map/ppermute | solution.py:12
  186.3 1.5 constant_dynamic-update-slice_fusion.4
  188.2 1.6 constant_dynamic-update-slice_fusion.1
  189.8 1.5 constant_dynamic-update-slice_fusion
  191.3 15.2 %convolution_convert_fusion = bf16[2048,2304]{1,0:T(8,128)(2,1)} fusion(bf16[1280,2304]{1,0:T(8,128)(2,1)S(1)} %bitcast.38, bf16[4096,1280]{0,1:T(8,128)(2,1)S(1)} %constant_dynamic-update-slice_fusion, s32[]{:T(128)S(6)} %select_n.62), kind=kOutput, calls=%fused_computation.1 | convolution fusion | flops 12084314112 | bytes 20578308 | tf_op jit(solution)/shard_map/dot_general | solution.py:60
  206.6 77.9 %reduce-scatter.2.cloned.1.call-done = bf16[256,2304]{1,0:T(8,128)(2,1)} async-done(((bf16[2048,2304]{1,0:T(8,128)(2,1)}), bf16[256,2304]{1,0:T(8,128)(2,1)}) %reduce-scatter.2.cloned.1.call-update) | async-done | bytes 1179664 | tf_op jit(solution)/shard_map/reduce_scatter | solution.py:59
  (29 shorter events, 1.4 us)
Async XLA Ops:
  6.5 31.1 %copy-start = (s32[6,2]{0,1:T(2,128)S(1)}, s32[6,2]{0,1:T(2,128)}, u32[]{:S(2)}) copy-start(s32[6,2]{0,1:T(2,128)} %param.7) | copy-start | bytes 148
  6.5 76.7 %all-gather.3.cloned.1.call-start = ((), (), s32[]{:S(2)}) async-start(), calls=%async_computation.1 | async-start | bytes 7077888 | tf_op jit(solution)/shard_map/all_gather | solution.py:51
  37.4 247.1 %reduce-scatter.2.cloned.1.call-start = ((), (), s32[]{:S(2)}) async-start(), calls=%async_computation.2 | async-start | bytes 10616832 | tf_op jit(solution)/shard_map/reduce_scatter | solution.py:59
  91.2 31.8 %collective-permute-start = (bf16[512,1280]{0,1:T(8,128)(2,1)S(1)}, bf16[512,1280]{0,1:T(8,128)(2,1)S(1)}, u32[]{:S(2)}, u32[]{:S(2)}) collective-permute-start(bf16[512,1280]{0,1:T(8,128)(2,1)S(1)} %bitcast.33), channel_id=1, source_target_pairs={{0,3},{1,0},{2,1},{3,2},{4,7},{5,4},{6,5},{7,6},{8,11},{9,8},{10,9... | collective-permute-start | bytes 3932168 | tf_op jit(solution)/shard_map/ppermute | solution.py:12
  123.0 31.9 %collective-permute-start.1 = (bf16[512,1280]{0,1:T(8,128)(2,1)S(1)}, bf16[512,1280]{0,1:T(8,128)(2,1)}, u32[]{:S(2)}, u32[]{:S(2)}) collective-permute-start(bf16[512,1280]{0,1:T(8,128)(2,1)S(1)} %collective-permute-done), channel_id=1, source_target_pairs={{0,3},{1,0},{2,1},{3,2},{4,7},{5,4},{6,5},{7,6},{8,11},{9,8},{10,9... | collective-permute-start | bytes 3932168 | tf_op jit(solution)/shard_map/ppermute | solution.py:12
  154.9 31.4 %collective-permute-start.2 = (bf16[512,1280]{0,1:T(8,128)(2,1)}, bf16[512,1280]{0,1:T(8,128)(2,1)}, u32[]{:S(2)}, u32[]{:S(2)}) collective-permute-start(bf16[512,1280]{0,1:T(8,128)(2,1)} %collective-permute-done.1), channel_id=1, source_target_pairs={{0,3},{1,0},{2,1},{3,2},{4,7},{5,4},{6,5},{7,6},{8,11},{9,8},{10,9... | collective-permute-start | bytes 3932168 | tf_op jit(solution)/shard_map/ppermute | solution.py:12
  159.4 31.8 %slice-start = ((s8[5898240]{0:T(1024)(128)(4,1)}), s8[4194304]{0:T(1024)(128)(4,1)S(1)}, s32[]{:S(2)}) async-start(s8[5898240]{0:T(1024)(128)(4,1)} %bitcast.37), calls=%async_computation.3 | async-start | bytes 8388608
  187.8 3.5 %slice-start.1 = ((s8[5898240]{0:T(1024)(128)(4,1)}), s8[1703936]{0:T(1024)(128)(4,1)S(1)}, s32[]{:S(2)}) async-start(s8[5898240]{0:T(1024)(128)(4,1)} %bitcast.37), calls=%async_computation.4 | async-start | bytes 3407872
Sparse Core Ops, SparseCore 0:
  37.5 45.6 all-gather.2
  206.7 77.7 reduce-scatter.1
